TPU v7x, 32 devices: a whole 2x2x4 slice. The times are simulated.
32 devices in a mesh: seq: 8 (over y, x, core), head: 4 (over z).
Axes of the slice: x: 2, y: 2, z: 4, core: 2. Of those that a mesh axis runs over, the one named last changes fastest.
Arguments:
- queries: bfloat16 [8, 32, 128], P('seq', 'head'), may hold values from -40 to 40
- key_pool: bfloat16 [288, 16, 128, 128], P('seq', 'head'), may hold values from -6 to 6
- value_pool: bfloat16 [288, 16, 128, 128], P('seq', 'head'), may hold values from -6 to 6
- lengths: int32 [8], replicated, may hold values from 2 to 16384, as said below
- block_table: int32 [8, 33], replicated, may hold values from -1 to 287, as said below
- out_weight: bfloat16 [4096, 4608], P('head'), may hold values from -0.09375 to 0.09375
Outputs:
- projected: bfloat16 [8, 4608], replicated
Inputs may be any that keep to these rules, and one draw needn't show every extreme that they name: `lengths`: at least 2; some request has exactly 16384. `block_table`: for request b the first (L - 1) // 128 - max(L - 4096, 0) // 128 + 1 entries hold slots; the rest are -1. No slot appears twice in the table.
All inputs are finite; a program needn't handle non-finite values.
Results may differ from a plain program's by a relative error of at most 0.017.
Values may be sent and summed in bfloat16 or wider, within the bound.
A program may use at most 64 MiB of HBM per device.

v0:
```python
import functools

import jax
import jax.numpy as jnp
from jax import lax
from jax.experimental import pallas as pl
from jax.experimental.pallas import tpu as pltpu
from jax.sharding import PartitionSpec as P

WINDOW = 4096

lowest_score = -1e30
lowest_largest = -1e29
score_scale = 1.0 / 12.0
LANES = 128
F32 = jnp.float32
BF16 = jnp.bfloat16
MESH = pl.DeviceIdType.MESH


def column_tiles(width, parts):
    tiles = width // LANES
    starts = [tiles * i // parts for i in range(parts)]
    ends = starts[1:] + [tiles]
    span = max(e - s for s, e in zip(starts, ends))
    return tiles, starts, ends, span


def peer_index(index, step, size):
    if size & (size - 1):
        return lax.rem(index + step, size)
    peer, bit = 0, 1
    while bit < size:
        own = lax.rem(lax.div(index, bit), 2)
        peer = peer + bit * ((1 - own) if step & bit else own)
        bit *= 2
    return peer


def kernel(
    n, nz,
    q_hbm, k_hbm, v_hbm, len_hbm, tab_hbm, w_hbm, out_ref,
    kbuf, vbuf, wbuf, qall, qf, tabv, lens, bias, scores, probs,
    mlbuf, obuf, wts, zbuf, fbuf,
    in_sem, k_sem, v_sem, q_send, q_recv, ml_send, ml_recv,
    o_send, o_recv, z_send, z_recv, f_send, f_recv,
):
    me = lax.axis_index("seq")
    mz = lax.axis_index("head")
    slot_count, kv_count, block_len, head_width = k_hbm.shape
    batch, entries = tab_hbm.shape
    own_batch, head_count = q_hbm.shape[0], q_hbm.shape[1]
    group = head_count // kv_count
    tiles, starts, ends, span = column_tiles(w_hbm.shape[1], n)
    total_columns = slot_count * block_len
    seq_peer = [peer_index(me, j, n) for j in range(n)]
    head_peer = [peer_index(mz, j, nz) for j in range(nz)]

    barrier = pltpu.get_barrier_semaphore()
    for j in reversed(range(1, n)):
        pl.semaphore_signal(barrier, inc=1, device_id={"seq": seq_peer[j]}, device_id_type=MESH)
    for j in reversed(range(1, nz)):
        pl.semaphore_signal(barrier, inc=1, device_id={"head": head_peer[j]}, device_id_type=MESH)

    own_rows = pl.ds(me * own_batch, own_batch)
    q_in = pltpu.make_async_copy(q_hbm, qall.at[own_rows], in_sem.at[0])
    tab_in = pltpu.make_async_copy(tab_hbm, tabv, in_sem.at[1])
    len_in = pltpu.make_async_copy(len_hbm, lens, in_sem.at[2])
    first_column = pl.multiple_of((tiles * me // n) * LANES, LANES)
    w_in = pltpu.make_async_copy(
        w_hbm.at[:, pl.ds(first_column, span * LANES)], wbuf, in_sem.at[3]
    )
    k_in = [pltpu.make_async_copy(k_hbm.at[:, k], kbuf.at[k], k_sem.at[k]) for k in range(kv_count)]
    v_in = [pltpu.make_async_copy(v_hbm.at[:, k], vbuf.at[k], v_sem.at[k]) for k in range(kv_count)]
    for copy in [q_in, tab_in, len_in] + k_in + v_in + [w_in]:
        copy.start()

    def to_seq(ref, send, recv):
        copies = []
        for j in reversed(range(1, n)):
            copies.append(
                pltpu.make_async_remote_copy(
                    src_ref=ref, dst_ref=ref, send_sem=send(j), recv_sem=recv(j),
                    device_id={"seq": seq_peer[j]}, device_id_type=MESH,
                )
            )
        for copy in copies:
            copy.start()
        return copies

    q_in.wait()
    pl.semaphore_wait(barrier, n - 1 + nz - 1)
    q_copies = to_seq(qall.at[own_rows], lambda j: q_send.at[j], lambda j: q_recv.at[j])

    tab_in.wait()
    len_in.wait()
    row = lax.broadcasted_iota(jnp.int32, (batch, LANES), 0)
    lane = lax.broadcasted_iota(jnp.int32, (batch, LANES), 1)
    length = jnp.zeros((batch, LANES), jnp.int32)
    for b in range(batch):
        length = jnp.where(row == b, lens[b], length)
    window_start = jnp.maximum(length - WINDOW, 0)
    first_block = lax.div(window_start, block_len)
    table = tabv[...]
    slot_lane = lane + me * slot_count
    rank = jnp.full((batch, LANES), -1, jnp.int32)
    for j in range(entries):
        rank = jnp.where(table[:, j : j + 1] == slot_lane, j, rank)
    base = (first_block + rank) * block_len
    low = jnp.where(rank >= 0, window_start - base, block_len)
    high = jnp.where(rank >= 0, length - base, 0)
    for p in range(slot_count):
        live = (lane >= low[:, p : p + 1]) & (lane < high[:, p : p + 1])
        bias[:, p * block_len : (p + 1) * block_len] = jnp.where(live, 0.0, lowest_score)

    for copy in k_in + v_in + [w_in]:
        copy.wait()
    for copy in q_copies:
        copy.wait_recv()
    for b in range(batch):
        qf[b * head_count : (b + 1) * head_count, :] = qall[b].astype(F32)

    chunk = 4 if slot_count % 4 == 0 else 1
    width = chunk * block_len
    chunks = slot_count // chunk
    rows = group * batch

    def lane_tiles(x, op):
        out = x[:, :LANES]
        for c in range(1, x.shape[1] // LANES):
            out = op(out, x[:, c * LANES : (c + 1) * LANES])
        return out

    largest, totals = [], []

    def score(k):
        grouped = jnp.concatenate(
            [qf[pl.ds(k * group + g, batch, stride=head_count), :] for g in range(group)], axis=0
        ).astype(BF16)
        top = jnp.full((rows, LANES), lowest_largest, F32)
        for c in range(chunks):
            keys = kbuf[k, c * chunk : (c + 1) * chunk].reshape(width, head_width)
            s = lax.dot_general(
                grouped, keys, (((1,), (1,)), ((), ())), preferred_element_type=F32
            )
            mask = bias[:, c * width : (c + 1) * width]
            s = s * score_scale + jnp.concatenate([mask] * group, axis=0)
            scores[k, :, c * width : (c + 1) * width] = s
            top = jnp.maximum(top, lane_tiles(s, jnp.maximum))
        largest.append(jnp.max(top, axis=1, keepdims=True))

    def soften(k):
        total = jnp.zeros((rows, LANES), F32)
        for c in range(chunks):
            weight = jnp.exp(scores[k, :, c * width : (c + 1) * width] - largest[k])
            total = total + lane_tiles(weight, jnp.add)
            probs[k, :, c * width : (c + 1) * width] = weight.astype(BF16)
        totals.append(jnp.sum(total, axis=1, keepdims=True))

    def share_totals():
        packed_largest = jnp.zeros((batch, LANES), F32)
        packed_total = jnp.ones((batch, LANES), F32)
        for k in range(kv_count):
            for g in range(group):
                h = k * group + g
                part = slice(g * batch, (g + 1) * batch)
                packed_largest = jnp.where(lane == h, largest[k][part], packed_largest)
                packed_total = jnp.where(lane == h, totals[k][part], packed_total)
        mlbuf[me, 0] = packed_largest
        mlbuf[me, 1] = packed_total
        return to_seq(mlbuf.at[me], lambda j: ml_send.at[j], lambda j: ml_recv.at[j])

    def share_sums(k):
        values = vbuf[k].reshape(total_columns, head_width)
        summed = jnp.dot(probs[k], values, preferred_element_type=F32)
        obuf[me, k] = summed.astype(BF16)
        return to_seq(obuf.at[me, k], lambda j: o_send.at[j, k], lambda j: o_recv.at[j, k])

    o_copies = []
    for k in range(kv_count):
        score(k)
    for k in range(kv_count):
        soften(k)
    ml_copies = share_totals()
    for k in range(kv_count):
        o_copies.append(share_sums(k))

    for copy in ml_copies:
        copy.wait_recv()
    whole_largest = mlbuf[0, 0]
    for i in range(1, n):
        whole_largest = jnp.maximum(whole_largest, mlbuf[i, 0])
    whole_total = jnp.zeros((batch, LANES), F32)
    factors = []
    for i in range(n):
        factors.append(jnp.exp(mlbuf[i, 0] - whole_largest))
        whole_total = whole_total + factors[i] * mlbuf[i, 1]
    inverse = 1.0 / whole_total
    for i in range(n):
        factor = factors[i] * inverse
        for h in range(head_count):
            wts[i, h] = jnp.broadcast_to(factor[:, h : h + 1], (batch, LANES))

    partial_sum = jnp.zeros((batch, span * LANES), F32)
    for k in range(kv_count):
        for copy in o_copies[k]:
            copy.wait_recv()
        parts = [jnp.zeros((batch, head_width), F32) for _ in range(group)]
        for i in range(n):
            arrived = obuf[i, k].astype(F32)
            for g in range(group):
                parts[g] = parts[g] + wts[i, k * group + g] * arrived[g * batch : (g + 1) * batch]
        attention = jnp.concatenate(parts, axis=1).astype(BF16)
        depth = group * head_width
        partial_sum = partial_sum + jnp.dot(
            attention, wbuf[k * depth : (k + 1) * depth, :], preferred_element_type=F32
        )

    zbuf[mz] = partial_sum.astype(BF16)
    z_copies = []
    for j in reversed(range(1, nz)):
        z_copies.append(
            pltpu.make_async_remote_copy(
                src_ref=zbuf.at[mz], dst_ref=zbuf.at[mz],
                send_sem=z_send.at[j], recv_sem=z_recv.at[j],
                device_id={"head": head_peer[j]}, device_id_type=MESH,
            )
        )
    for copy in z_copies:
        copy.start()
    for copy in z_copies:
        copy.wait_recv()
    finished = zbuf[0].astype(F32)
    for i in range(1, nz):
        finished = finished + zbuf[i].astype(F32)
    fbuf[me] = finished.astype(BF16)
    f_copies = to_seq(fbuf.at[me], lambda j: f_send.at[j], lambda j: f_recv.at[j])
    for copy in f_copies:
        copy.wait_recv()
    for i in range(n):
        if ends[i] > starts[i]:
            out_ref[:, starts[i] * LANES : ends[i] * LANES] = fbuf[
                i, :, : (ends[i] - starts[i]) * LANES
            ]
    for copy in q_copies + ml_copies + z_copies + f_copies:
        copy.wait_send()
    for copies in o_copies:
        for copy in copies:
            copy.wait_send()


def local(n, nz, queries, key_pool, value_pool, lengths, block_table, out_weight):
    slot_count, kv_count, block_len, head_width = key_pool.shape
    batch, entries = block_table.shape
    head_count = queries.shape[1]
    rows = head_count // kv_count * batch
    columns = slot_count * block_len
    depth, out_width = out_weight.shape
    _, _, _, span = column_tiles(out_width, n)
    dma = pltpu.SemaphoreType.DMA
    hbm = pl.BlockSpec(memory_space=pl.ANY)
    return pl.pallas_call(
        functools.partial(kernel, n, nz),
        out_shape=pltpu.VMEM((batch, out_width), BF16),
        in_specs=[hbm] * 6,
        out_specs=pl.BlockSpec(memory_space=pltpu.VMEM),
        scratch_shapes=[
            pltpu.VMEM((kv_count, slot_count, block_len, head_width), BF16),
            pltpu.VMEM((kv_count, slot_count, block_len, head_width), BF16),
            pltpu.VMEM((depth, span * LANES), BF16),
            pltpu.VMEM((batch, head_count, head_width), BF16),
            pltpu.VMEM((batch * head_count, head_width), F32),
            pltpu.VMEM((batch, entries), jnp.int32),
            pltpu.SMEM((batch,), jnp.int32),
            pltpu.VMEM((batch, columns), F32),
            pltpu.VMEM((kv_count, rows, columns), F32),
            pltpu.VMEM((kv_count, rows, columns), BF16),
            pltpu.VMEM((n, 2, batch, LANES), F32),
            pltpu.VMEM((n, kv_count, rows, head_width), BF16),
            pltpu.VMEM((n, head_count, batch, LANES), F32),
            pltpu.VMEM((nz, batch, span * LANES), BF16),
            pltpu.VMEM((n, batch, span * LANES), BF16),
            dma((4,)), dma((kv_count,)), dma((kv_count,)),
            dma((n,)), dma((n,)), dma((n,)), dma((n,)),
            dma((n, kv_count)), dma((n, kv_count)),
            dma((nz,)), dma((nz,)), dma((n,)), dma((n,)),
        ],
        compiler_params=pltpu.CompilerParams(
            collective_id=0, has_side_effects=True, vmem_limit_bytes=56 * 1024 * 1024
        ),
    )(queries, key_pool, value_pool, lengths, block_table, out_weight)


def solution(mesh):
    return jax.shard_map(
        functools.partial(local, mesh.shape["seq"], mesh.shape["head"]),
        mesh=mesh,
        in_specs=(
            P("seq", "head", None),
            P("seq", "head", None, None),
            P("seq", "head", None, None),
            P(),
            P(),
            P("head", None),
        ),
        out_specs=P(),
        check_vma=False,
    )
```

profile of v0, /device:TPU:0, one launch (start us, length us, event | category | flops | bytes accessed | tf_op | source)
XLA Modules:
  0.0 22.9 jit_solution(3155948884095551564)
XLA Ops:
  0.0 22.3 %shard_map.64 = bf16[8,4608]{1,0:T(8,128)(2,1)S(1)} custom-call(bf16[1,8,128]{2,1,0:T(8,128)(2,1)} %q_hbm.1, bf16[36,4,128,128]{3,2,1,0:T(8,128)(2,1)} %k_hbm.1, bf16[36,4,128,128]{3,2,1,0:T(8,128)(2,1)} %v_hbm.1, s32[8]{0:T(128)} %len_hbm.1, s32[8,33]{1,0:T(8,128)} %tab_hbm.1, bf16[1024,4608]{1,0:T(8,128)(2,1)} %w_hbm.1), custom_call_target="tpu_custom_call" | custom-call | tf_op jit(solution)/shard_map/pallas_call | solution.py:262
  22.3 0.6 %copy.8 = bf16[8,4608]{1,0:T(8,128)(2,1)} copy(bf16[8,4608]{1,0:T(8,128)(2,1)S(1)} %shard_map.64) | data formatting | bytes 147456
where the time goes:
time: 23.1 us; the launch traced here: 22.9 us
  Pallas kernels  22.3 us (97%)
  local copies, waits for them, and re-layouts  0.64 us (3%)
    pallas_call x1, Pallas kernels, local(): pl.pallas_call(functools.partial(kernel, n, nz), out_shape=pltpu.VMEM((ba...  22.3 us
    unnamed x1, local copies, waits for them, and re-layouts  0.64 us

commit v1 on v0

--- a/solution.py
+++ b/solution.py
@@ -43,7 +43,7 @@
     kbuf, vbuf, wbuf, qall, qf, tabv, lens, bias, scores, probs,
     mlbuf, obuf, wts, zbuf, fbuf,
     in_sem, k_sem, v_sem, q_send, q_recv, ml_send, ml_recv,
-    o_send, o_recv, z_send, z_recv, f_send, f_recv,
+    o_send, o_recv, z_send, z_recv, f_send, f_recv, seq_ready, head_ready,
 ):
     me = lax.axis_index("seq")
     mz = lax.axis_index("head")
@@ -57,10 +57,21 @@
     head_peer = [peer_index(mz, j, nz) for j in range(nz)]
 
     barrier = pltpu.get_barrier_semaphore()
+    greets_seq = lax.rem(me, 2) == 1
+    partner = seq_peer[1]
+    others = [lax.rem(mz + j, nz) for j in range(1, nz)]
+    chip = me - lax.rem(me, 2)
     for j in reversed(range(1, n)):
-        pl.semaphore_signal(barrier, inc=1, device_id={"seq": seq_peer[j]}, device_id_type=MESH)
-    for j in reversed(range(1, nz)):
-        pl.semaphore_signal(barrier, inc=1, device_id={"head": head_peer[j]}, device_id_type=MESH)
+        peer = seq_peer[j]
+
+        @pl.when(lax.rem(peer, 2) == 1)
+        def _():
+            pl.semaphore_signal(barrier, inc=1, device_id={"seq": peer}, device_id_type=MESH)
+
+    for z in others:
+        pl.semaphore_signal(
+            barrier, inc=1, device_id={"seq": chip, "head": z}, device_id_type=MESH
+        )
 
     own_rows = pl.ds(me * own_batch, own_batch)
     q_in = pltpu.make_async_copy(q_hbm, qall.at[own_rows], in_sem.at[0])
@@ -72,7 +83,11 @@
     )
     k_in = [pltpu.make_async_copy(k_hbm.at[:, k], kbuf.at[k], k_sem.at[k]) for k in range(kv_count)]
     v_in = [pltpu.make_async_copy(v_hbm.at[:, k], vbuf.at[k], v_sem.at[k]) for k in range(kv_count)]
-    for copy in [q_in, tab_in, len_in] + k_in + v_in + [w_in]:
+    for copy in [q_in, tab_in, len_in]:
+        copy.start()
+    for copy in [q_in, tab_in, len_in]:
+        copy.wait()
+    for copy in k_in + v_in + [w_in]:
         copy.start()
 
     def to_seq(ref, send, recv):
@@ -88,12 +103,17 @@
             copy.start()
         return copies
 
-    q_in.wait()
-    pl.semaphore_wait(barrier, n - 1 + nz - 1)
+    @pl.when(greets_seq)
+    def _():
+        pl.semaphore_wait(barrier, n - 1)
+        pl.semaphore_signal(seq_ready, inc=1, device_id={"seq": partner}, device_id_type=MESH)
+
+    @pl.when(jnp.logical_not(greets_seq))
+    def _():
+        pl.semaphore_wait(seq_ready, 1)
+
     q_copies = to_seq(qall.at[own_rows], lambda j: q_send.at[j], lambda j: q_recv.at[j])
 
-    tab_in.wait()
-    len_in.wait()
     row = lax.broadcasted_iota(jnp.int32, (batch, LANES), 0)
     lane = lax.broadcasted_iota(jnp.int32, (batch, LANES), 1)
     length = jnp.zeros((batch, LANES), jnp.int32)
@@ -215,6 +235,15 @@
         partial_sum = partial_sum + jnp.dot(
             attention, wbuf[k * depth : (k + 1) * depth, :], preferred_element_type=F32
         )
+
+    @pl.when(jnp.logical_not(greets_seq))
+    def _():
+        pl.semaphore_wait(barrier, 2 * (nz - 1))
+        pl.semaphore_signal(head_ready, inc=1, device_id={"seq": partner}, device_id_type=MESH)
+
+    @pl.when(greets_seq)
+    def _():
+        pl.semaphore_wait(head_ready, 1)
 
     zbuf[mz] = partial_sum.astype(BF16)
     z_copies = []
@@ -284,6 +313,7 @@
             dma((n,)), dma((n,)), dma((n,)), dma((n,)),
             dma((n, kv_count)), dma((n, kv_count)),
             dma((nz,)), dma((nz,)), dma((n,)), dma((n,)),
+            pltpu.SemaphoreType.REGULAR, pltpu.SemaphoreType.REGULAR,
         ],
         compiler_params=pltpu.CompilerParams(
             collective_id=0, has_side_effects=True, vmem_limit_bytes=56 * 1024 * 1024

time: 23.1 us -> 23.5 us (1.017)
  Pallas kernels: 22.3 us -> 22.7 us
    pallas_call x1, Pallas kernels: 22.3 us -> 22.7 us  [local(): pl.pallas_call(functools.partial(kernel, n, nz), out_shape=pltpu.VMEM((ba...]
where the time goes in v1:
time: 23.5 us; the launch traced here: 23.4 us
  Pallas kernels  22.7 us (97%)
  local copies, waits for them, and re-layouts  0.64 us (3%)
    pallas_call x1, Pallas kernels, local(): pl.pallas_call(functools.partial(kernel, n, nz), out_shape=pltpu.VMEM((ba...  22.7 us
    unnamed x1, local copies, waits for them, and re-layouts  0.64 us

profile of v1, /device:TPU:0, one launch (start us, length us, event | category | flops | bytes accessed | tf_op | source)
XLA Modules:
  0.0 23.4 jit_solution(10829630093349888086)
XLA Ops:
  0.0 22.7 %shard_map.64 = bf16[8,4608]{1,0:T(8,128)(2,1)S(1)} custom-call(bf16[1,8,128]{2,1,0:T(8,128)(2,1)} %q_hbm.1, bf16[36,4,128,128]{3,2,1,0:T(8,128)(2,1)} %k_hbm.1, bf16[36,4,128,128]{3,2,1,0:T(8,128)(2,1)} %v_hbm.1, s32[8]{0:T(128)} %len_hbm.1, s32[8,33]{1,0:T(8,128)} %tab_hbm.1, bf16[1024,4608]{1,0:T(8,128)(2,1)} %w_hbm.1), custom_call_target="tpu_custom_call" | custom-call | tf_op jit(solution)/shard_map/pallas_call | solution.py:291
  22.7 0.6 %copy.8 = bf16[8,4608]{1,0:T(8,128)(2,1)} copy(bf16[8,4608]{1,0:T(8,128)(2,1)S(1)} %shard_map.64) | data formatting | bytes 147456

commit v2 on v0

v2 whole, which is shorter than its diff:
```python
import functools

import jax
import jax.numpy as jnp
from jax import lax
from jax.experimental import pallas as pl
from jax.experimental.pallas import tpu as pltpu
from jax.sharding import PartitionSpec as P

WINDOW = 4096

lowest_score = -1e30
lowest_largest = -1e29
score_scale = 1.0 / 12.0
LANES = 128
F32 = jnp.float32
BF16 = jnp.bfloat16
MESH = pl.DeviceIdType.MESH


def column_tiles(width, parts):
    tiles = width // LANES
    starts = [tiles * i // parts for i in range(parts)]
    ends = starts[1:] + [tiles]
    span = max(e - s for s, e in zip(starts, ends))
    return tiles, starts, ends, span


def batch_split(n, batch):
    return 2 if n % 2 == 0 and batch % 2 == 0 else 1


def peer_index(index, step, size):
    if size & (size - 1):
        return lax.rem(index + step, size)
    peer, bit = 0, 1
    while bit < size:
        own = lax.rem(lax.div(index, bit), 2)
        peer = peer + bit * ((1 - own) if step & bit else own)
        bit *= 2
    return peer


def kernel(
    n, nz,
    q_hbm, k_hbm, v_hbm, len_hbm, tab_hbm, w_hbm, out_ref,
    kbuf, vbuf, wbuf, kflip, qall, qf, tabv, lens, bias, scores, probs,
    mlown, mlbuf, oown, obuf, wts, zbuf, fbuf,
    in_sem, k_sem, q_sem, ml_sem, o_send, o_recv, z_sem, f_sem,
):
    me = lax.axis_index("seq")
    mz = lax.axis_index("head")
    slot_count, kv_count, block_len, head_width = k_hbm.shape
    batch, entries = tab_hbm.shape
    own_batch, head_count = q_hbm.shape[0], q_hbm.shape[1]
    group = head_count // kv_count
    split = batch_split(n, batch)
    parts, share = n // split, batch // split
    rows = group * share
    tiles, starts, ends, span = column_tiles(w_hbm.shape[1], parts)
    total_columns = slot_count * block_len
    seq_peer = [peer_index(me, j, n) for j in range(n)]
    head_peer = [peer_index(mz, j, nz) for j in range(nz)]

    barrier = pltpu.get_barrier_semaphore()
    for j in reversed(range(1, n)):
        pl.semaphore_signal(barrier, inc=1, device_id={"seq": seq_peer[j]}, device_id_type=MESH)
    for j in reversed(range(1, nz)):
        pl.semaphore_signal(barrier, inc=1, device_id={"head": head_peer[j]}, device_id_type=MESH)

    own_rows = pl.ds(me * own_batch, own_batch)
    q_in = pltpu.make_async_copy(q_hbm, qall.at[own_rows], in_sem.at[0])
    tab_in = pltpu.make_async_copy(tab_hbm, tabv, in_sem.at[1])
    len_in = pltpu.make_async_copy(len_hbm, lens, in_sem.at[2])
    first_column = pl.multiple_of((tiles * lax.div(me, split) // parts) * LANES, LANES)
    w_in = pltpu.make_async_copy(
        w_hbm.at[:, pl.ds(first_column, span * LANES)], wbuf, in_sem.at[3]
    )
    k_in = [pltpu.make_async_copy(k_hbm.at[:, k], kbuf.at[k], k_sem.at[k]) for k in range(kv_count)]
    v_in = [pltpu.make_async_copy(v_hbm.at[:, k], vbuf.at[k], in_sem.at[4]) for k in range(kv_count)]
    for copy in [q_in, tab_in, len_in]:
        copy.start()
    for copy in [q_in, tab_in, len_in]:
        copy.wait()
    for copy in k_in + v_in + [w_in]:
        copy.start()

    def to_seq(source, target, send, recv):
        copies = []
        for j in reversed(range(1, n)):
            copies.append(
                pltpu.make_async_remote_copy(
                    src_ref=source(seq_peer[j]), dst_ref=target, send_sem=send, recv_sem=recv,
                    device_id={"seq": seq_peer[j]}, device_id_type=MESH,
                )
            )
        for copy in copies:
            copy.start()

    def wait_all(ref, sem):
        pltpu.make_async_copy(ref, ref, sem).wait()

    pl.semaphore_wait(barrier, n - 1 + nz - 1)
    to_seq(lambda peer: qall.at[own_rows], qall.at[own_rows], q_sem.at[0], q_sem.at[1])

    def by_rows(x):
        return jnp.concatenate(
            [x[s * share : (s + 1) * share] for s in range(split) for _ in range(group)], axis=0
        )

    all_rows = split * rows
    row = lax.broadcasted_iota(jnp.int32, (batch, LANES), 0)
    lane = lax.broadcasted_iota(jnp.int32, (batch, LANES), 1)
    length = jnp.zeros((batch, LANES), jnp.int32)
    for b in range(batch):
        length = jnp.where(row == b, lens[b], length)
    window_start = jnp.maximum(length - WINDOW, 0)
    first_block = lax.div(window_start, block_len)
    table = tabv[...]
    slot_lane = lane + me * slot_count
    rank = jnp.full((batch, LANES), -1, jnp.int32)
    for j in range(entries):
        rank = jnp.where(table[:, j : j + 1] == slot_lane, j, rank)
    base = (first_block + rank) * block_len
    low = by_rows(jnp.where(rank >= 0, window_start - base, block_len))
    high = by_rows(jnp.where(rank >= 0, length - base, 0))
    lane = lax.broadcasted_iota(jnp.int32, (all_rows, LANES), 1)
    for p in range(slot_count):
        live = (lane >= low[:, p : p + 1]) & (lane < high[:, p : p + 1])
        bias[:, p * block_len : (p + 1) * block_len] = jnp.where(live, 0.0, lowest_score)

    for k in range(kv_count):
        k_in[k].wait()
        for p in range(slot_count):
            kflip[k, :, p * block_len : (p + 1) * block_len] = kbuf[k, p].T

    wait_all(vbuf, in_sem.at[4])
    wait_all(qall.at[pl.ds(0, (n - 1) * own_batch)], q_sem.at[1])
    for b in range(batch):
        qf[b * head_count : (b + 1) * head_count, :] = qall[b].astype(F32)

    chunk = 4 if slot_count % 4 == 0 else 1
    width = chunk * block_len
    chunks = slot_count // chunk

    def lane_tiles(x, op):
        out = x[:, :LANES]
        for c in range(1, x.shape[1] // LANES):
            out = op(out, x[:, c * LANES : (c + 1) * LANES])
        return out

    largest, totals = [], []

    def score(k):
        grouped = jnp.concatenate(
            [
                qf[pl.ds(s * share * head_count + k * group + g, share, stride=head_count), :]
                for s in range(split)
                for g in range(group)
            ],
            axis=0,
        ).astype(BF16)
        top = jnp.full((all_rows, LANES), lowest_largest, F32)
        for c in range(chunks):
            part = slice(c * width, (c + 1) * width)
            s = jnp.dot(grouped, kflip[k, :, part], preferred_element_type=F32)
            s = s * score_scale + bias[:, part]
            scores[k, :, part] = s
            top = jnp.maximum(top, lane_tiles(s, jnp.maximum))
        largest.append(jnp.max(top, axis=1, keepdims=True))

    def soften(k):
        total = jnp.zeros((all_rows, LANES), F32)
        for c in range(chunks):
            part = slice(c * width, (c + 1) * width)
            weight = jnp.exp(scores[k, :, part] - largest[k])
            total = total + lane_tiles(weight, jnp.add)
            probs[k, :, part] = weight.astype(BF16)
        totals.append(jnp.sum(total, axis=1, keepdims=True))

    own_share = lax.rem(me, split)

    def share_totals():
        packed = jnp.ones((all_rows, LANES), F32)
        for k in range(kv_count):
            packed = jnp.where(lane == k, largest[k], packed)
            packed = jnp.where(lane == kv_count + k, totals[k], packed)
        for s in range(split):
            mlown[s] = packed[s * rows : (s + 1) * rows]
        mlbuf[me] = mlown[own_share]
        to_seq(
            lambda peer: mlown.at[lax.rem(peer, split)], mlbuf.at[me], ml_sem.at[0], ml_sem.at[1]
        )

    def share_sums(k):
        values = vbuf[k].reshape(total_columns, head_width)
        summed = jnp.dot(probs[k], values, preferred_element_type=F32).astype(BF16)
        for s in range(split):
            oown[k, s] = summed[s * rows : (s + 1) * rows]
        obuf[k, me] = oown[k, own_share]
        to_seq(
            lambda peer: oown.at[k, lax.rem(peer, split)], obuf.at[k, me], o_send.at[0], o_recv.at[k]
        )

    for k in range(kv_count):
        score(k)
    for k in range(kv_count):
        soften(k)
    share_totals()
    for k in range(kv_count):
        share_sums(k)

    others = pl.ds(0, n - 1)
    wait_all(mlbuf.at[others], ml_sem.at[1])
    whole_largest = mlbuf[0]
    for i in range(1, n):
        whole_largest = jnp.maximum(whole_largest, mlbuf[i])
    whole_total = jnp.zeros((rows, LANES), F32)
    factors = []
    for i in range(n):
        factors.append(jnp.exp(jnp.minimum(mlbuf[i] - whole_largest, 0.0)))
        whole_total = whole_total + factors[i] * pltpu.roll(mlbuf[i], LANES - kv_count, 1)
    inverse = 1.0 / whole_total
    for i in range(n):
        factor = factors[i] * inverse
        for k in range(kv_count):
            wts[i, k] = jnp.broadcast_to(factor[:, k : k + 1], (rows, head_width))

    w_in.wait()
    partial_sum = jnp.zeros((share, span * LANES), F32)
    depth = group * head_width
    for k in range(kv_count):
        wait_all(obuf.at[k, others], o_recv.at[k])
        part = jnp.zeros((rows, head_width), F32)
        for i in range(n):
            part = part + wts[i, k] * obuf[k, i].astype(F32)
        attention = jnp.concatenate(
            [part[g * share : (g + 1) * share] for g in range(group)], axis=1
        ).astype(BF16)
        partial_sum = partial_sum + jnp.dot(
            attention, wbuf[k * depth : (k + 1) * depth, :], preferred_element_type=F32
        )

    zbuf[mz] = partial_sum.astype(BF16)
    for j in reversed(range(1, nz)):
        pltpu.make_async_remote_copy(
            src_ref=zbuf.at[mz], dst_ref=zbuf.at[mz], send_sem=z_sem.at[0], recv_sem=z_sem.at[1],
            device_id={"head": head_peer[j]}, device_id_type=MESH,
        ).start()
    wait_all(zbuf.at[pl.ds(0, nz - 1)], z_sem.at[1])
    finished = zbuf[0].astype(F32)
    for z in range(1, nz):
        finished = finished + zbuf[z].astype(F32)
    fbuf[me] = finished.astype(BF16)
    to_seq(lambda peer: fbuf.at[me], fbuf.at[me], f_sem.at[0], f_sem.at[1])
    wait_all(fbuf.at[others], f_sem.at[1])
    for c in range(parts):
        if ends[c] > starts[c]:
            filled = (ends[c] - starts[c]) * LANES
            out_ref[:, starts[c] * LANES : ends[c] * LANES] = jnp.concatenate(
                [fbuf[c * split + s, :, :filled] for s in range(split)], axis=0
            )
    wait_all(qall.at[pl.ds(0, (n - 1) * own_batch)], q_sem.at[0])
    wait_all(mlbuf.at[others], ml_sem.at[0])
    wait_all(obuf.at[:, others], o_send.at[0])
    wait_all(zbuf.at[pl.ds(0, nz - 1)], z_sem.at[0])
    wait_all(fbuf.at[others], f_sem.at[0])


def local(n, nz, queries, key_pool, value_pool, lengths, block_table, out_weight):
    slot_count, kv_count, block_len, head_width = key_pool.shape
    batch, entries = block_table.shape
    head_count = queries.shape[1]
    split = batch_split(n, batch)
    share = batch // split
    rows = head_count // kv_count * share
    columns = slot_count * block_len
    depth, out_width = out_weight.shape
    _, _, _, span = column_tiles(out_width, n // split)
    dma = pltpu.SemaphoreType.DMA
    hbm = pl.BlockSpec(memory_space=pl.ANY)
    return pl.pallas_call(
        functools.partial(kernel, n, nz),
        out_shape=pltpu.VMEM((batch, out_width), BF16),
        in_specs=[hbm] * 6,
        out_specs=pl.BlockSpec(memory_space=pltpu.VMEM),
        scratch_shapes=[
            pltpu.VMEM((kv_count, slot_count, block_len, head_width), BF16),
            pltpu.VMEM((kv_count, slot_count, block_len, head_width), BF16),
            pltpu.VMEM((depth, span * LANES), BF16),
            pltpu.VMEM((kv_count, head_width, columns), BF16),
            pltpu.VMEM((batch, head_count, head_width), BF16),
            pltpu.VMEM((batch * head_count, head_width), F32),
            pltpu.VMEM((batch, entries), jnp.int32),
            pltpu.SMEM((batch,), jnp.int32),
            pltpu.VMEM((split * rows, columns), F32),
            pltpu.VMEM((kv_count, split * rows, columns), F32),
            pltpu.VMEM((kv_count, split * rows, columns), BF16),
            pltpu.VMEM((split, rows, LANES), F32),
            pltpu.VMEM((n, rows, LANES), F32),
            pltpu.VMEM((kv_count, split, rows, head_width), BF16),
            pltpu.VMEM((kv_count, n, rows, head_width), BF16),
            pltpu.VMEM((n, kv_count, rows, head_width), F32),
            pltpu.VMEM((nz, share, span * LANES), BF16),
            pltpu.VMEM((n, share, span * LANES), BF16),
            dma((5,)), dma((kv_count,)), dma((2,)), dma((2,)),
            dma((1,)), dma((kv_count,)), dma((2,)), dma((2,)),
        ],
        compiler_params=pltpu.CompilerParams(
            collective_id=0, has_side_effects=True, vmem_limit_bytes=56 * 1024 * 1024
        ),
    )(queries, key_pool, value_pool, lengths, block_table, out_weight)


def solution(mesh):
    return jax.shard_map(
        functools.partial(local, mesh.shape["seq"], mesh.shape["head"]),
        mesh=mesh,
        in_specs=(
            P("seq", "head", None),
            P("seq", "head", None, None),
            P("seq", "head", None, None),
            P(),
            P(),
            P("head", None),
        ),
        out_specs=P(),
        check_vma=False,
    )
```

time: 23.1 us -> 21.5 us (0.931)
  Pallas kernels: 22.3 us -> 20.7 us
    pallas_call x1, Pallas kernels: 22.3 us -> 20.7 us  [local(): pl.pallas_call(functools.partial(kernel, n, nz), out_shape=pltpu.VMEM((ba...]
where the time goes in v2:
time: 21.5 us; the launch traced here: 21.4 us
  Pallas kernels  20.7 us (96%)
  local copies, waits for them, and re-layouts  0.64 us (3%)
    pallas_call x1, Pallas kernels, local(): pl.pallas_call(functools.partial(kernel, n, nz), out_shape=pltpu.VMEM((ba...  20.7 us
    unnamed x1, local copies, waits for them, and re-layouts  0.64 us

profile of v2, /device:TPU:0, one launch (start us, length us, event | category | flops | bytes accessed | tf_op | source)
XLA Modules:
  0.0 21.4 jit_solution(5466059050173715301)
XLA Ops:
  0.0 20.7 %shard_map.64 = bf16[8,4608]{1,0:T(8,128)(2,1)S(1)} custom-call(bf16[1,8,128]{2,1,0:T(8,128)(2,1)} %q_hbm.1, bf16[36,4,128,128]{3,2,1,0:T(8,128)(2,1)} %k_hbm.1, bf16[36,4,128,128]{3,2,1,0:T(8,128)(2,1)} %v_hbm.1, s32[8]{0:T(128)} %len_hbm.1, s32[8,33]{1,0:T(8,128)} %tab_hbm.1, bf16[1024,4608]{1,0:T(8,128)(2,1)} %w_hbm.1), custom_call_target="tpu_custom_call" | custom-call | tf_op jit(solution)/shard_map/pallas_call | solution.py:282
  20.7 0.6 %copy.8 = bf16[8,4608]{1,0:T(8,128)(2,1)} copy(bf16[8,4608]{1,0:T(8,128)(2,1)S(1)} %shard_map.64) | data formatting | bytes 147456

commit v3 on v2

v3 whole, which is shorter than its diff:
```python
import functools

import jax
import jax.numpy as jnp
from jax import lax
from jax.experimental import pallas as pl
from jax.experimental.pallas import tpu as pltpu
from jax.sharding import PartitionSpec as P

WINDOW = 4096

lowest_score = -1e30
lowest_largest = -1e29
score_scale = 1.0 / 12.0
LANES = 128
F32 = jnp.float32
BF16 = jnp.bfloat16
MESH = pl.DeviceIdType.MESH


def column_tiles(width, parts):
    tiles = width // LANES
    starts = [tiles * i // parts for i in range(parts)]
    ends = starts[1:] + [tiles]
    span = max(e - s for s, e in zip(starts, ends))
    return tiles, starts, ends, span


def cores_of(n):
    return 2 if n % 2 == 0 else 1


def peer_index(index, step, size):
    if size & (size - 1):
        return lax.rem(index + step, size)
    peer, bit = 0, 1
    while bit < size:
        own = lax.rem(lax.div(index, bit), 2)
        peer = peer + bit * ((1 - own) if step & bit else own)
        bit *= 2
    return peer


def kernel(
    n, nz,
    q_hbm, k_hbm, v_hbm, len_hbm, tab_hbm, w_hbm, out_ref,
    kbuf, vbuf, wbuf, kflip, qall, qf, tabv, lens, bias, scores, probs,
    mlbuf, obuf, wts, zbuf, fbuf,
    in_sem, k_sem, q_sem, ml_sem, o_send, o_recv, z_sem, f_sem,
):
    me = lax.axis_index("seq")
    mz = lax.axis_index("head")
    slot_count, kv_count, block_len, head_width = k_hbm.shape
    batch, entries = tab_hbm.shape
    own_batch, head_count = q_hbm.shape[0], q_hbm.shape[1]
    group = head_count // kv_count
    cores = cores_of(n)
    parts, part = n // cores, lax.div(me, cores)
    rows = group * batch
    tiles, starts, ends, span = column_tiles(w_hbm.shape[1], parts)

    def owns(index):
        return lax.rem(index, cores) == cores - 1

    total_columns = slot_count * block_len
    seq_peer = [peer_index(me, j, n) for j in range(n)]
    head_peer = [peer_index(mz, j, nz) for j in range(nz)]

    barrier = pltpu.get_barrier_semaphore()
    for j in reversed(range(1, n)):
        pl.semaphore_signal(barrier, inc=1, device_id={"seq": seq_peer[j]}, device_id_type=MESH)

    @pl.when(owns(me))
    def _():
        for j in reversed(range(1, nz)):
            pl.semaphore_signal(
                barrier, inc=1, device_id={"head": head_peer[j]}, device_id_type=MESH
            )

    own_rows = pl.ds(me * own_batch, own_batch)
    q_in = pltpu.make_async_copy(q_hbm, qall.at[own_rows], in_sem.at[0])
    tab_in = pltpu.make_async_copy(tab_hbm, tabv, in_sem.at[1])
    len_in = pltpu.make_async_copy(len_hbm, lens, in_sem.at[2])
    first_column = pl.multiple_of((tiles * part // parts) * LANES, LANES)
    w_in = pltpu.make_async_copy(
        w_hbm.at[:, pl.ds(first_column, span * LANES)], wbuf, in_sem.at[3]
    )
    k_in = [pltpu.make_async_copy(k_hbm.at[:, k], kbuf.at[k], k_sem.at[k]) for k in range(kv_count)]
    v_in = [pltpu.make_async_copy(v_hbm.at[:, k], vbuf.at[k], in_sem.at[4]) for k in range(kv_count)]
    for copy in [q_in, tab_in, len_in]:
        copy.start()
    for copy in [q_in, tab_in, len_in]:
        copy.wait()
    for copy in k_in + v_in:
        copy.start()
    pl.when(owns(me))(w_in.start)

    def to_seq(source, target, send, recv, to_owners=False):
        for j in reversed(range(1, n)):
            copy = pltpu.make_async_remote_copy(
                src_ref=source, dst_ref=target, send_sem=send, recv_sem=recv,
                device_id={"seq": seq_peer[j]}, device_id_type=MESH,
            )
            if to_owners:
                pl.when(owns(seq_peer[j]))(copy.start)
            else:
                copy.start()

    def wait_all(ref, sem):
        pltpu.make_async_copy(ref, ref, sem).wait()

    pl.semaphore_wait(barrier, n - 1 + jnp.where(owns(me), nz - 1, 0))
    to_seq(qall.at[own_rows], qall.at[own_rows], q_sem.at[0], q_sem.at[1])

    row = lax.broadcasted_iota(jnp.int32, (batch, LANES), 0)
    lane = lax.broadcasted_iota(jnp.int32, (batch, LANES), 1)
    length = jnp.zeros((batch, LANES), jnp.int32)
    for b in range(batch):
        length = jnp.where(row == b, lens[b], length)
    window_start = jnp.maximum(length - WINDOW, 0)
    first_block = lax.div(window_start, block_len)
    table = tabv[...]
    slot_lane = lane + me * slot_count
    rank = jnp.full((batch, LANES), -1, jnp.int32)
    for j in range(entries):
        rank = jnp.where(table[:, j : j + 1] == slot_lane, j, rank)
    base = (first_block + rank) * block_len
    low = jnp.where(rank >= 0, window_start - base, block_len)
    high = jnp.where(rank >= 0, length - base, 0)
    for p in range(slot_count):
        live = (lane >= low[:, p : p + 1]) & (lane < high[:, p : p + 1])
        bias[:, p * block_len : (p + 1) * block_len] = jnp.where(live, 0.0, lowest_score)

    for k in range(kv_count):
        k_in[k].wait()
        for p in range(slot_count):
            kflip[k, :, p * block_len : (p + 1) * block_len] = kbuf[k, p].T

    wait_all(vbuf, in_sem.at[4])
    wait_all(qall.at[pl.ds(0, (n - 1) * own_batch)], q_sem.at[1])
    for b in range(batch):
        qf[b * head_count : (b + 1) * head_count, :] = qall[b].astype(F32)

    chunk = 4 if slot_count % 4 == 0 else 1
    width = chunk * block_len
    chunks = slot_count // chunk

    def lane_tiles(x, op):
        out = x[:, :LANES]
        for c in range(1, x.shape[1] // LANES):
            out = op(out, x[:, c * LANES : (c + 1) * LANES])
        return out

    largest, totals = [], []

    def score(k):
        grouped = jnp.concatenate(
            [qf[pl.ds(k * group + g, batch, stride=head_count), :] for g in range(group)], axis=0
        ).astype(BF16)
        top = jnp.full((rows, LANES), lowest_largest, F32)
        for c in range(chunks):
            piece = slice(c * width, (c + 1) * width)
            s = jnp.dot(grouped, kflip[k, :, piece], preferred_element_type=F32)
            s = s * score_scale + jnp.concatenate([bias[:, piece]] * group, axis=0)
            scores[k, :, piece] = s
            top = jnp.maximum(top, lane_tiles(s, jnp.maximum))
        largest.append(jnp.max(top, axis=1, keepdims=True))

    def soften(k):
        total = jnp.zeros((rows, LANES), F32)
        for c in range(chunks):
            piece = slice(c * width, (c + 1) * width)
            weight = jnp.exp(scores[k, :, piece] - largest[k])
            total = total + lane_tiles(weight, jnp.add)
            probs[k, :, piece] = weight.astype(BF16)
        totals.append(jnp.sum(total, axis=1, keepdims=True))

    def share_totals():
        packed = jnp.ones((batch, LANES), F32)
        for k in range(kv_count):
            for g in range(group):
                h = k * group + g
                own = slice(g * batch, (g + 1) * batch)
                packed = jnp.where(lane == h, largest[k][own], packed)
                packed = jnp.where(lane == head_count + h, totals[k][own], packed)
        mlbuf[me] = packed
        to_seq(mlbuf.at[me], mlbuf.at[me], ml_sem.at[0], ml_sem.at[1], to_owners=True)

    def share_sums(k):
        values = vbuf[k].reshape(total_columns, head_width)
        obuf[k, me] = jnp.dot(probs[k], values, preferred_element_type=F32).astype(BF16)
        to_seq(obuf.at[k, me], obuf.at[k, me], o_send.at[0], o_recv.at[k], to_owners=True)

    for k in range(kv_count):
        score(k)
    for k in range(kv_count):
        soften(k)
    share_totals()
    for k in range(kv_count):
        share_sums(k)

    others = pl.ds(0, n - 1)

    @pl.when(owns(me))
    def _():
        wait_all(mlbuf.at[others], ml_sem.at[1])
        whole_largest = mlbuf[0]
        for i in range(1, n):
            whole_largest = jnp.maximum(whole_largest, mlbuf[i])
        whole_total = jnp.zeros((batch, LANES), F32)
        factors = []
        for i in range(n):
            factors.append(jnp.exp(mlbuf[i] - whole_largest))
            whole_total = whole_total + factors[i] * pltpu.roll(mlbuf[i], LANES - head_count, 1)
        inverse = 1.0 / whole_total
        for i in range(n):
            factor = factors[i] * inverse
            for h in range(head_count):
                wts[i, h] = jnp.broadcast_to(factor[:, h : h + 1], (batch, head_width))

        w_in.wait()
        partial_sum = jnp.zeros((batch, span * LANES), F32)
        depth = group * head_width
        for k in range(kv_count):
            wait_all(obuf.at[k, others], o_recv.at[k])
            sums = [jnp.zeros((batch, head_width), F32) for _ in range(group)]
            for i in range(n):
                arrived = obuf[k, i].astype(F32)
                for g in range(group):
                    own = slice(g * batch, (g + 1) * batch)
                    sums[g] = sums[g] + wts[i, k * group + g] * arrived[own]
            attention = jnp.concatenate(sums, axis=1).astype(BF16)
            partial_sum = partial_sum + jnp.dot(
                attention, wbuf[k * depth : (k + 1) * depth, :], preferred_element_type=F32
            )

        zbuf[mz] = partial_sum.astype(BF16)
        for j in reversed(range(1, nz)):
            pltpu.make_async_remote_copy(
                src_ref=zbuf.at[mz], dst_ref=zbuf.at[mz], send_sem=z_sem.at[0], recv_sem=z_sem.at[1],
                device_id={"head": head_peer[j]}, device_id_type=MESH,
            ).start()
        wait_all(zbuf.at[pl.ds(0, nz - 1)], z_sem.at[1])
        finished = zbuf[0].astype(F32)
        for z in range(1, nz):
            finished = finished + zbuf[z].astype(F32)
        fbuf[part] = finished.astype(BF16)
        to_seq(fbuf.at[part], fbuf.at[part], f_sem.at[0], f_sem.at[1])
        if parts > 1:
            wait_all(fbuf.at[pl.ds(0, parts - 1)], f_sem.at[1])

    if cores > 1:

        @pl.when(jnp.logical_not(owns(me)))
        def _():
            wait_all(fbuf.at[pl.ds(0, parts)], f_sem.at[1])

    for c in range(parts):
        if ends[c] > starts[c]:
            filled = (ends[c] - starts[c]) * LANES
            out_ref[:, starts[c] * LANES : ends[c] * LANES] = fbuf[c, :, :filled]
    wait_all(qall.at[pl.ds(0, (n - 1) * own_batch)], q_sem.at[0])

    @pl.when(owns(me))
    def _():
        if parts > 1:
            wait_all(mlbuf.at[pl.ds(0, parts - 1)], ml_sem.at[0])
            wait_all(obuf.at[:, pl.ds(0, parts - 1)], o_send.at[0])
        wait_all(zbuf.at[pl.ds(0, nz - 1)], z_sem.at[0])
        wait_all(fbuf.at[others], f_sem.at[0])

    if cores > 1:

        @pl.when(jnp.logical_not(owns(me)))
        def _():
            wait_all(mlbuf.at[pl.ds(0, parts)], ml_sem.at[0])
            wait_all(obuf.at[:, pl.ds(0, parts)], o_send.at[0])


def local(n, nz, queries, key_pool, value_pool, lengths, block_table, out_weight):
    slot_count, kv_count, block_len, head_width = key_pool.shape
    batch, entries = block_table.shape
    head_count = queries.shape[1]
    rows = head_count // kv_count * batch
    columns = slot_count * block_len
    depth, out_width = out_weight.shape
    _, _, _, span = column_tiles(out_width, n // cores_of(n))
    dma = pltpu.SemaphoreType.DMA
    hbm = pl.BlockSpec(memory_space=pl.ANY)
    return pl.pallas_call(
        functools.partial(kernel, n, nz),
        out_shape=pltpu.VMEM((batch, out_width), BF16),
        in_specs=[hbm] * 6,
        out_specs=pl.BlockSpec(memory_space=pltpu.VMEM),
        scratch_shapes=[
            pltpu.VMEM((kv_count, slot_count, block_len, head_width), BF16),
            pltpu.VMEM((kv_count, slot_count, block_len, head_width), BF16),
            pltpu.VMEM((depth, span * LANES), BF16),
            pltpu.VMEM((kv_count, head_width, columns), BF16),
            pltpu.VMEM((batch, head_count, head_width), BF16),
            pltpu.VMEM((batch * head_count, head_width), F32),
            pltpu.VMEM((batch, entries), jnp.int32),
            pltpu.SMEM((batch,), jnp.int32),
            pltpu.VMEM((batch, columns), F32),
            pltpu.VMEM((kv_count, rows, columns), F32),
            pltpu.VMEM((kv_count, rows, columns), BF16),
            pltpu.VMEM((n, batch, LANES), F32),
            pltpu.VMEM((kv_count, n, rows, head_width), BF16),
            pltpu.VMEM((n, head_count, batch, head_width), F32),
            pltpu.VMEM((nz, batch, span * LANES), BF16),
            pltpu.VMEM((n, batch, span * LANES), BF16),
            dma((5,)), dma((kv_count,)), dma((2,)), dma((2,)),
            dma((1,)), dma((kv_count,)), dma((2,)), dma((2,)),
        ],
        compiler_params=pltpu.CompilerParams(
            collective_id=0, has_side_effects=True, vmem_limit_bytes=56 * 1024 * 1024
        ),
    )(queries, key_pool, value_pool, lengths, block_table, out_weight)


def solution(mesh):
    return jax.shard_map(
        functools.partial(local, mesh.shape["seq"], mesh.shape["head"]),
        mesh=mesh,
        in_specs=(
            P("seq", "head", None),
            P("seq", "head", None, None),
            P("seq", "head", None, None),
            P(),
            P(),
            P("head", None),
        ),
        out_specs=P(),
        check_vma=False,
    )
```

time: 21.5 us -> 20 us (0.930)
  Pallas kernels: 20.7 us -> 19.2 us
    pallas_call x1, Pallas kernels: 20.7 us -> 19.2 us  [local(): pl.pallas_call(functools.partial(kernel, n, nz), out_shape=pltpu.VMEM((ba...]
where the time goes in v3:
time: 20 us; the launch traced here: 19.9 us
  Pallas kernels  19.2 us (96%)
  local copies, waits for them, and re-layouts  0.64 us (3%)
    pallas_call x1, Pallas kernels, local(): pl.pallas_call(functools.partial(kernel, n, nz), out_shape=pltpu.VMEM((ba...  19.2 us
    unnamed x1, local copies, waits for them, and re-layouts  0.64 us

profile of v3, /device:TPU:0, one launch (start us, length us, event | category | flops | bytes accessed | tf_op | source)
XLA Modules:
  0.0 19.9 jit_solution(9104994717620219074)
XLA Ops:
  0.0 19.2 %shard_map.64 = bf16[8,4608]{1,0:T(8,128)(2,1)S(1)} custom-call(bf16[1,8,128]{2,1,0:T(8,128)(2,1)} %q_hbm.1, bf16[36,4,128,128]{3,2,1,0:T(8,128)(2,1)} %k_hbm.1, bf16[36,4,128,128]{3,2,1,0:T(8,128)(2,1)} %v_hbm.1, s32[8]{0:T(128)} %len_hbm.1, s32[8,33]{1,0:T(8,128)} %tab_hbm.1, bf16[1024,4608]{1,0:T(8,128)(2,1)} %w_hbm.1), custom_call_target="tpu_custom_call" | custom-call | tf_op jit(solution)/shard_map/pallas_call | solution.py:290
  19.2 0.6 %copy.8 = bf16[8,4608]{1,0:T(8,128)(2,1)} copy(bf16[8,4608]{1,0:T(8,128)(2,1)S(1)} %shard_map.64) | data formatting | bytes 147456

commit v4 on v3

--- a/solution.py
+++ b/solution.py
@@ -89,22 +89,25 @@
     v_in = [pltpu.make_async_copy(v_hbm.at[:, k], vbuf.at[k], in_sem.at[4]) for k in range(kv_count)]
     for copy in [q_in, tab_in, len_in]:
         copy.start()
-    for copy in [q_in, tab_in, len_in]:
-        copy.wait()
-    for copy in k_in + v_in:
+    q_in.wait()
+    for copy in k_in:
         copy.start()
-    pl.when(owns(me))(w_in.start)
 
     def to_seq(source, target, send, recv, to_owners=False):
-        for j in reversed(range(1, n)):
-            copy = pltpu.make_async_remote_copy(
+        def copy(index):
+            return pltpu.make_async_remote_copy(
                 src_ref=source, dst_ref=target, send_sem=send, recv_sem=recv,
-                device_id={"seq": seq_peer[j]}, device_id_type=MESH,
+                device_id={"seq": index}, device_id_type=MESH,
             )
-            if to_owners:
-                pl.when(owns(seq_peer[j]))(copy.start)
-            else:
-                copy.start()
+
+        if not to_owners:
+            for j in reversed(range(1, n)):
+                copy(seq_peer[j]).start()
+            return
+        for j in reversed(range(1, parts)):
+            copy(peer_index(part, j, parts) * cores + cores - 1).start()
+        if cores > 1:
+            pl.when(jnp.logical_not(owns(me)))(copy(part * cores + cores - 1).start)
 
     def wait_all(ref, sem):
         pltpu.make_async_copy(ref, ref, sem).wait()
@@ -112,6 +115,8 @@
     pl.semaphore_wait(barrier, n - 1 + jnp.where(owns(me), nz - 1, 0))
     to_seq(qall.at[own_rows], qall.at[own_rows], q_sem.at[0], q_sem.at[1])
 
+    tab_in.wait()
+    len_in.wait()
     row = lax.broadcasted_iota(jnp.int32, (batch, LANES), 0)
     lane = lax.broadcasted_iota(jnp.int32, (batch, LANES), 1)
     length = jnp.zeros((batch, LANES), jnp.int32)
@@ -133,10 +138,11 @@
 
     for k in range(kv_count):
         k_in[k].wait()
+        v_in[k].start()
         for p in range(slot_count):
             kflip[k, :, p * block_len : (p + 1) * block_len] = kbuf[k, p].T
 
-    wait_all(vbuf, in_sem.at[4])
+    pl.when(owns(me))(w_in.start)
     wait_all(qall.at[pl.ds(0, (n - 1) * own_batch)], q_sem.at[1])
     for b in range(batch):
         qf[b * head_count : (b + 1) * head_count, :] = qall[b].astype(F32)
@@ -196,6 +202,7 @@
     for k in range(kv_count):
         soften(k)
     share_totals()
+    wait_all(vbuf, in_sem.at[4])
     for k in range(kv_count):
         share_sums(k)
 

time: 20 us -> 19.6 us (0.980)
  Pallas kernels: 19.2 us -> 18.8 us
    pallas_call x1, Pallas kernels: 19.2 us -> 18.8 us  [local(): pl.pallas_call(functools.partial(kernel, n, nz), out_shape=pltpu.VMEM((ba...]
where the time goes in v4:
time: 19.6 us; the launch traced here: 19.5 us
  Pallas kernels  18.8 us (96%)
  local copies, waits for them, and re-layouts  0.64 us (3%)
    pallas_call x1, Pallas kernels, local(): pl.pallas_call(functools.partial(kernel, n, nz), out_shape=pltpu.VMEM((ba...  18.8 us
    unnamed x1, local copies, waits for them, and re-layouts  0.64 us

profile of v4, /device:TPU:0, one launch (start us, length us, event | category | flops | bytes accessed | tf_op | source)
XLA Modules:
  0.0 19.5 jit_solution(13774505831532432396)
XLA Ops:
  0.0 18.8 %shard_map.64 = bf16[8,4608]{1,0:T(8,128)(2,1)S(1)} custom-call(bf16[1,8,128]{2,1,0:T(8,128)(2,1)} %q_hbm.1, bf16[36,4,128,128]{3,2,1,0:T(8,128)(2,1)} %k_hbm.1, bf16[36,4,128,128]{3,2,1,0:T(8,128)(2,1)} %v_hbm.1, s32[8]{0:T(128)} %len_hbm.1, s32[8,33]{1,0:T(8,128)} %tab_hbm.1, bf16[1024,4608]{1,0:T(8,128)(2,1)} %w_hbm.1), custom_call_target="tpu_custom_call" | custom-call | tf_op jit(solution)/shard_map/pallas_call | solution.py:297
  18.8 0.6 %copy.8 = bf16[8,4608]{1,0:T(8,128)(2,1)} copy(bf16[8,4608]{1,0:T(8,128)(2,1)S(1)} %shard_map.64) | data formatting | bytes 147456

commit v5 on v4

--- a/solution.py
+++ b/solution.py
@@ -46,7 +46,7 @@
     q_hbm, k_hbm, v_hbm, len_hbm, tab_hbm, w_hbm, out_ref,
     kbuf, vbuf, wbuf, kflip, qall, qf, tabv, lens, bias, scores, probs,
     mlbuf, obuf, wts, zbuf, fbuf,
-    in_sem, k_sem, q_sem, ml_sem, o_send, o_recv, z_sem, f_sem,
+    in_sem, k_sem, v_sem, q_sem, ml_sem, o_send, o_recv, z_sem, f_sem,
 ):
     me = lax.axis_index("seq")
     mz = lax.axis_index("head")
@@ -86,7 +86,7 @@
         w_hbm.at[:, pl.ds(first_column, span * LANES)], wbuf, in_sem.at[3]
     )
     k_in = [pltpu.make_async_copy(k_hbm.at[:, k], kbuf.at[k], k_sem.at[k]) for k in range(kv_count)]
-    v_in = [pltpu.make_async_copy(v_hbm.at[:, k], vbuf.at[k], in_sem.at[4]) for k in range(kv_count)]
+    v_in = [pltpu.make_async_copy(v_hbm.at[:, k], vbuf.at[k], v_sem.at[k]) for k in range(kv_count)]
     for copy in [q_in, tab_in, len_in]:
         copy.start()
     q_in.wait()
@@ -202,8 +202,8 @@
     for k in range(kv_count):
         soften(k)
     share_totals()
-    wait_all(vbuf, in_sem.at[4])
     for k in range(kv_count):
+        v_in[k].wait()
         share_sums(k)
 
     others = pl.ds(0, n - 1)
@@ -316,7 +316,7 @@
             pltpu.VMEM((n, head_count, batch, head_width), F32),
             pltpu.VMEM((nz, batch, span * LANES), BF16),
             pltpu.VMEM((n, batch, span * LANES), BF16),
-            dma((5,)), dma((kv_count,)), dma((2,)), dma((2,)),
+            dma((4,)), dma((kv_count,)), dma((kv_count,)), dma((2,)), dma((2,)),
             dma((1,)), dma((kv_count,)), dma((2,)), dma((2,)),
         ],
         compiler_params=pltpu.CompilerParams(

time: 19.6 us -> 19.7 us (level)
  no operation moved by 1% of the time
where the time goes in v5:
time: 19.7 us; the launch traced here: 19.5 us
  Pallas kernels  18.9 us (96%)
  local copies, waits for them, and re-layouts  0.64 us (3%)
    pallas_call x1, Pallas kernels, local(): pl.pallas_call(functools.partial(kernel, n, nz), out_shape=pltpu.VMEM((ba...  18.9 us
    unnamed x1, local copies, waits for them, and re-layouts  0.64 us

profile of v5, /device:TPU:0, one launch (start us, length us, event | category | flops | bytes accessed | tf_op | source)
XLA Modules:
  0.0 19.5 jit_solution(6340777713117521822)
XLA Ops:
  0.0 18.9 %shard_map.64 = bf16[8,4608]{1,0:T(8,128)(2,1)S(1)} custom-call(bf16[1,8,128]{2,1,0:T(8,128)(2,1)} %q_hbm.1, bf16[36,4,128,128]{3,2,1,0:T(8,128)(2,1)} %k_hbm.1, bf16[36,4,128,128]{3,2,1,0:T(8,128)(2,1)} %v_hbm.1, s32[8]{0:T(128)} %len_hbm.1, s32[8,33]{1,0:T(8,128)} %tab_hbm.1, bf16[1024,4608]{1,0:T(8,128)(2,1)} %w_hbm.1), custom_call_target="tpu_custom_call" | custom-call | tf_op jit(solution)/shard_map/pallas_call | solution.py:297
  18.9 0.6 %copy.8 = bf16[8,4608]{1,0:T(8,128)(2,1)} copy(bf16[8,4608]{1,0:T(8,128)(2,1)S(1)} %shard_map.64) | data formatting | bytes 147456
